TPU v7x, 32 devices: a whole 2x2x4 slice. The times are simulated.
32 devices in a mesh: tok: 4 (over z), out: 4 (over x, core), grp: 2 (over y).
Axes of the slice: x: 2, y: 2, z: 4, core: 2. Of those that a mesh axis runs over, the one named last changes fastest.
Arguments:
- activations: bfloat16 [1024, 2, 2048], P(('tok', 'grp'), None, 'out'), may hold values from -16 to 16
- out_grads: bfloat16 [1024, 2, 2048], P(('tok', 'grp'), None, 'out'), may hold values from -16 to 16
- weight: bfloat16 [2, 2048, 4096], P(None, 'out'), may hold values from -0.09375 to 0.09375
Outputs:
- update: bfloat16 [4096, 2, 2048], P(('tok', 'grp'), None, 'out')
- input_grad: bfloat16 [1024, 2, 2048], P(('tok', 'grp'), None, 'out')
All inputs are finite; a program needn't handle non-finite values.
Results may differ from a plain program's by a relative error of at most 0.0092.
Values may be sent and summed in bfloat16 or wider, within the bound.
A program may use at most 64 MiB of HBM per device.

v0:
```python
import math
import jax
import jax.numpy as jnp
from jax import lax
from jax.sharding import PartitionSpec as P

POWER = 3
DAMPING = 0.1
HIGH = lax.Precision.HIGHEST


def spread(piece):
    return lax.all_gather(piece, "out", axis=2, tiled=True)


def token_sums(maker, rows):
    return lax.psum_scatter(
        maker(jnp.int32(0), rows * lax.axis_size(("tok", "grp"))),
        ("tok", "grp"),
        scatter_dimension=0,
        tiled=True,
    )


def shared_rows(piece):
    return lax.all_gather(piece, ("tok", "grp"), axis=0, tiled=True)


def shared_total(vector):
    return lax.psum(vector, ("tok", "out", "grp"))


def diagonal_mask(rows, width, row_start, col_start):
    row_ids = row_start + lax.broadcasted_iota(jnp.int32, (rows, 1, width), 0)
    col_ids = col_start + lax.broadcasted_iota(jnp.int32, (rows, 1, width), 2)
    return jnp.where(row_ids == col_ids, 1.0, 0.0).astype(jnp.float32)


def multiply(left, right, gather_columns):
    row_band = spread(left)
    column_band = gather_columns(right)
    return jnp.einsum("rkj,jkc->rkc", row_band, column_band, preferred_element_type=jnp.float32)


def inverse_roots(tile, row_start, col_start, gather_columns, total):
    rows, count, width = tile.shape
    block = width * lax.axis_size("out")
    mask = diagonal_mask(rows, width, row_start, col_start)
    vector = jnp.ones((count, block), jnp.float32)
    image = vector
    for step in range(POWER):
        columns = lax.dynamic_slice_in_dim(vector, col_start, width, 1)
        part = jnp.einsum("rkc,kc->kr", tile, columns, precision=HIGH)
        placed = lax.dynamic_update_slice_in_dim(
            jnp.zeros((count, block), jnp.float32), part, row_start, 1
        )
        image = total(placed)
        if step + 1 < POWER:
            vector = image / jnp.sqrt(jnp.sum(image * image, axis=1, keepdims=True))
    scale = jnp.sum(vector * image, axis=1) / jnp.sum(vector * vector, axis=1)
    start = tile / scale[None, :, None]
    start_low = start.astype(jnp.bfloat16)
    first_low = ((3.0 * mask - start) / 2.0).astype(jnp.bfloat16)
    square_low = multiply(first_low, first_low, gather_columns).astype(jnp.bfloat16)
    moved = multiply(square_low, start_low, gather_columns)
    second_low = ((3.0 * mask - moved) / 2.0).astype(jnp.bfloat16)
    roots = multiply(first_low, second_low, gather_columns) / jnp.sqrt(scale)[None, :, None]
    return roots.astype(jnp.bfloat16)


def local(activations, out_grads, weight):
    tok_dev, blocks, width = activations.shape
    block = width * lax.axis_size("out")
    token_count = tok_dev * lax.axis_size("tok") * lax.axis_size("grp")
    col_start = lax.axis_index("out") * width
    local_sides = jnp.concatenate([activations, out_grads], axis=1)
    whole_sides = spread(local_sides)
    grads_whole = whole_sides[:, blocks:, :]
    weight_rows = weight.reshape(blocks, width, blocks, block)
    input_grad = jnp.einsum(
        "tjq,bcjq->tbc", grads_whole, weight_rows, preferred_element_type=jnp.float32
    ).astype(jnp.bfloat16)
    rows = block // (lax.axis_size("tok") * lax.axis_size("grp"))
    row_start = lax.axis_index(("tok", "grp")) * rows

    def shared_terms(start, span):
        return jnp.einsum(
            "tkr,tkc->rkc", whole_sides, local_sides, preferred_element_type=jnp.float32
        )

    sums = token_sums(shared_terms, rows)
    tile = sums / token_count + DAMPING * diagonal_mask(rows, width, row_start, col_start)
    roots = inverse_roots(tile, row_start, col_start, shared_rows, shared_total)
    bands = shared_rows(roots)
    whitened = jnp.einsum(
        "tkj,jkc->tkc", whole_sides, bands, preferred_element_type=jnp.float32
    ).astype(jnp.bfloat16)
    acts_whole = spread(whitened[:, :blocks, :]).reshape(tok_dev, blocks * block)
    grads_low = whitened[:, blocks:, :]
    owned_acts = lax.all_to_all(acts_whole, ("tok", "grp"), split_axis=1, concat_axis=0, tiled=True)
    update = jnp.einsum(
        "ta,tbc->abc",
        owned_acts,
        lax.all_gather(grads_low, ("tok", "grp"), axis=0, tiled=True),
        preferred_element_type=jnp.float32,
    )
    update = (update / math.sqrt(token_count)).astype(jnp.bfloat16)
    return (update, input_grad)


def solution(mesh):
    in_specs = (
        P(("tok", "grp"), None, "out"),
        P(("tok", "grp"), None, "out"),
        P(None, "out", None),
    )
    out_specs = (P(("tok", "grp"), None, "out"), P(("tok", "grp"), None, "out"))
    return jax.shard_map(local, mesh=mesh, in_specs=in_specs, out_specs=out_specs, check_vma=False)
```

profile of v0, /device:TPU:0, one launch (start us, length us, event | category | flops | bytes accessed | tf_op | source)
XLA Modules:
  0.0 1136.9 jit_solution(8817919165431428209)
XLA Ops:
  7.2 0.0 all-gather.10.cloned.1.call-start
  7.2 1.0 copy_dynamic-update-slice_fusion.1
  8.2 1.0 copy_dynamic-update-slice_fusion
  9.2 0.0 copy-start.1
  9.2 0.8 copy-done.1
  10.0 0.0 all-gather.10.cloned.1.call-update
  10.0 0.0 reduce-scatter.2.cloned.1.call-start
  10.0 25.4 %all-gather.10.cloned.1.call-done = bf16[128,4,2048]{2,0,1:T(8,128)(2,1)} async-done(((bf16[128,4,512]{2,0,1:T(8,128)(2,1)}), bf16[128,4,2048]{2,0,1:T(8,128)(2,1)}) %all-gather.10.cloned.1.call-update) | async-done | bytes 2097168 | tf_op jit(solution)/shard_map/all_gather | solution.py:13
  35.4 9.9 convolution_bitcast_fusion
  45.3 0.0 reduce-scatter.2.cloned.1.call-update
  45.3 0.0 all-gather.16.cloned.1.call-start
  45.4 0.1 select_multiply_fusion.1
  45.6 280.1 %reduce-scatter.2.cloned.1.call-done = f32[256,4,512]{0,2,1:T(8,128)} async-done(((f32[2048,4,512]{0,2,1:T(8,128)}), f32[256,4,512]{0,2,1:T(8,128)}) %reduce-scatter.2.cloned.1.call-update) | async-done | bytes 2097168 | tf_op jit(solution)/shard_map/reduce_scatter | solution.py:17
  325.7 0.0 copy-start
  325.7 3.0 fusion.10
  328.7 39.4 %psum.21 = f32[4,2048]{1,0:T(4,128)S(1)} all-reduce(f32[4,2048]{1,0:T(4,128)S(1)} %bitcast_dynamic-update-slice_fusion.2), channel_id=1, replica_groups=mesh['tok'=4,'out'=4,'grp'=2] {'tok','out','grp'}, use_global_device_ids=true, to_apply=%region_1.2 | all-reduce | flops 8192 | bytes 65536 | tf_op jit(solution)/shard_map/psum | solution.py:30
  368.2 0.1 multiply_reduce_fusion.3
  368.3 0.1 fusion.26
  368.4 0.0 copy-done
  368.4 1.3 fusion.9
  369.8 39.9 %psum.22 = f32[4,2048]{1,0:T(4,128)S(1)} all-reduce(f32[4,2048]{1,0:T(4,128)S(1)} %bitcast_dynamic-update-slice_fusion.1), channel_id=1, replica_groups=mesh['tok'=4,'out'=4,'grp'=2] {'tok','out','grp'}, use_global_device_ids=true, to_apply=%region_3.4 | all-reduce | flops 8192 | bytes 65536 | tf_op jit(solution)/shard_map/psum | solution.py:30
  409.7 0.1 multiply_reduce_fusion.2
  409.9 0.1 broadcast_divide_fusion
  409.9 1.3 fusion.8
  411.3 40.3 %psum.23 = f32[4,2048]{1,0:T(4,128)S(1)} all-reduce(f32[4,2048]{1,0:T(4,128)S(1)} %bitcast_dynamic-update-slice_fusion), channel_id=1, replica_groups=mesh['tok'=4,'out'=4,'grp'=2] {'tok','out','grp'}, use_global_device_ids=true, to_apply=%region_5.6 | all-reduce | flops 8192 | bytes 65536 | tf_op jit(solution)/shard_map/psum | solution.py:30
  451.6 0.2 multiply_reduce_fusion
  451.8 1.8 multiply_convert_fusion.1
  453.6 0.0 all-gather.16.cloned.1.call-update
  453.6 0.0 all-gather.14.cloned.1.call-start
  453.7 0.5 all-gather.14.cloned.1.call-update
  454.2 0.0 all-gather.12.cloned.1.call-start
  454.2 0.5 all-gather.12.cloned.1.call-update
  454.8 0.0 all-gather.18.cloned.1.call-start
  454.8 33.2 %all-gather.16.cloned.1.call-done = bf16[256,4,2048]{0,2,1:T(8,128)(2,1)} async-done(((bf16[256,4,512]{0,2,1:T(8,128)(2,1)}), bf16[256,4,2048]{0,2,1:T(8,128)(2,1)}) %all-gather.16.cloned.1.call-update) | async-done | bytes 4194320 | tf_op jit(solution)/shard_map/all_gather | solution.py:13
  488.0 127.4 %all-gather.14.cloned.1.call-done = bf16[2048,4,512]{0,2,1:T(8,128)(2,1)} async-done(((bf16[256,4,512]{0,2,1:T(8,128)(2,1)}), bf16[2048,4,512]{0,2,1:T(8,128)(2,1)}) %all-gather.14.cloned.1.call-update) | async-done | bytes 8388624 | tf_op jit(solution)/shard_map/all_gather | solution.py:26
  615.5 7.9 fusion.5
  623.3 0.0 all-gather.18.cloned.1.call-update
  623.4 0.2 all-gather.20.cloned.1.call-start
  623.6 116.9 %all-gather.12.cloned.1.call-done = bf16[2048,4,512]{0,2,1:T(8,128)(2,1)} async-done(((bf16[256,4,512]{0,2,1:T(8,128)(2,1)}), bf16[2048,4,512]{0,2,1:T(8,128)(2,1)}) %all-gather.12.cloned.1.call-update) | async-done | bytes 8388624 | tf_op jit(solution)/shard_map/all_gather | solution.py:26
  740.5 34.7 %all-gather.18.cloned.1.call-done = bf16[256,4,2048]{0,2,1:T(8,128)(2,1)} async-done(((bf16[256,4,512]{0,2,1:T(8,128)(2,1)}), bf16[256,4,2048]{0,2,1:T(8,128)(2,1)}) %all-gather.18.cloned.1.call-update) | async-done | bytes 4194320 | tf_op jit(solution)/shard_map/all_gather | solution.py:13
  775.2 7.9 fusion.4
  783.0 0.0 all-gather.20.cloned.1.call-update
  783.1 0.0 all-gather.22.cloned.1.call-start
  783.1 125.0 %all-gather.20.cloned.1.call-done = bf16[2048,4,512]{0,2,1:T(8,128)(2,1)} async-done(((bf16[256,4,512]{0,2,1:T(8,128)(2,1)}), bf16[2048,4,512]{0,2,1:T(8,128)(2,1)}) %all-gather.20.cloned.1.call-update) | async-done | bytes 8388624 | tf_op jit(solution)/shard_map/all_gather | solution.py:26
  908.2 8.0 fusion.6
  916.2 0.0 all-gather.22.cloned.1.call-update
  916.2 0.0 all-gather.24.cloned.1.call-start
  916.3 123.2 %all-gather.22.cloned.1.call-done = bf16[2048,4,512]{0,2,1:T(8,128)(2,1)} async-done(((bf16[256,4,512]{0,2,1:T(8,128)(2,1)}), bf16[2048,4,512]{0,2,1:T(8,128)(2,1)}) %all-gather.22.cloned.1.call-update) | async-done | bytes 8388624 | tf_op jit(solution)/shard_map/all_gather | solution.py:26
  1039.5 0.0 copy-done.2
  1039.5 5.7 fusion.11
  1045.2 0.8 fusion.34
  1046.0 0.0 all-gather.24.cloned.1.call-update
  1046.1 0.0 all-gather.26.cloned.1.call-start
  1046.1 0.5 all-gather.26.cloned.1.call-update
  1046.6 14.4 %all-gather.24.cloned.1.call-done = bf16[128,2,2048]{0,2,1:T(8,128)(2,1)} async-done(((bf16[128,2,512]{0,2,1:T(8,128)(2,1)}), bf16[128,2,2048]{0,2,1:T(8,128)(2,1)}) %all-gather.24.cloned.1.call-update) | async-done | bytes 1048592 | tf_op jit(solution)/shard_map/all_gather | solution.py:13
  1061.1 5.5 all-to-all-start
  1066.6 6.3 fusion.15
  1072.9 1.0 copy.20
  1073.8 27.3 %all-to-all-done = bf16[128,8,512]{0,2,1:T(8,128)(2,1)S(1)} async-done(((bf16[128,8,512]{0,2,1:T(8,128)(2,1)}), bf16[128,8,512]{0,2,1:T(8,128)(2,1)S(1)}, u32[]{:S(2)}, u32[]{:S(2)}) %all-to-all-start) | async-done | bytes 1048608 | tf_op jit(solution)/shard_map/all_to_all | solution.py:100
  1101.2 0.7 copy.16
  1101.9 0.5 reshape.81
  1102.4 22.7 %all-gather.26.cloned.1.call-done = bf16[1024,2,512]{0,2,1:T(8,128)(2,1)} async-done(((bf16[128,2,512]{0,2,1:T(8,128)(2,1)}), bf16[1024,2,512]{0,2,1:T(8,128)(2,1)}) %all-gather.26.cloned.1.call-update) | async-done | bytes 2097168 | tf_op jit(solution)/shard_map/all_gather | solution.py:104
  1125.1 2.9 multiply_convert_fusion
  1128.0 2.0 copy.19
  (13 shorter events, 0.1 us)
Async XLA Ops:
  7.2 28.3 %all-gather.10.cloned.1.call-start = ((), (), s32[]{:S(2)}) async-start(), calls=%async_computation.2 | async-start | bytes 2621440 | tf_op jit(solution)/shard_map/all_gather | solution.py:13
  9.2 0.8 copy-start.1
  10.0 315.7 %reduce-scatter.2.cloned.1.call-start = ((), (), s32[]{:S(2)}) async-start(), calls=%async_computation.3 | async-start | bytes 18874368 | tf_op jit(solution)/shard_map/reduce_scatter | solution.py:17
  45.3 442.7 %all-gather.16.cloned.1.call-start = ((), (), s32[]{:S(2)}) async-start(), calls=%async_computation.6 | async-start | bytes 5242880 | tf_op jit(solution)/shard_map/all_gather | solution.py:13
  325.7 42.7 %copy-start = (f32[256,4,512]{0,2,1:T(8,128)S(1)}, f32[256,4,512]{0,2,1:T(8,128)}, u32[]{:S(2)}) copy-start(f32[256,4,512]{0,2,1:T(8,128)} %reduce-scatter.2.cloned.1.call-done) | copy-start | bytes 6291460
  453.6 161.9 %all-gather.14.cloned.1.call-start = ((), (), s32[]{:S(2)}) async-start(), calls=%async_computation.5 | async-start | bytes 9437184 | tf_op jit(solution)/shard_map/all_gather | solution.py:26
  454.2 286.3 %all-gather.12.cloned.1.call-start = ((), (), s32[]{:S(2)}) async-start(), calls=%async_computation.4 | async-start | bytes 9437184 | tf_op jit(solution)/shard_map/all_gather | solution.py:26
  454.8 320.4 %all-gather.18.cloned.1.call-start = ((), (), s32[]{:S(2)}) async-start(), calls=%async_computation.7 | async-start | bytes 5242880 | tf_op jit(solution)/shard_map/all_gather | solution.py:13
  623.4 284.8 %all-gather.20.cloned.1.call-start = ((), (), s32[]{:S(2)}) async-start(), calls=%async_computation.8 | async-start | bytes 9437184 | tf_op jit(solution)/shard_map/all_gather | solution.py:26
  783.1 256.4 %all-gather.22.cloned.1.call-start = ((), (), s32[]{:S(2)}) async-start(), calls=%async_computation.9 | async-start | bytes 9437184 | tf_op jit(solution)/shard_map/all_gather | solution.py:26
  908.2 131.3 %copy-start.2 = (bf16[128,4,2048]{2,0,1:T(8,128)(2,1)S(1)}, bf16[128,4,2048]{2,0,1:T(8,128)(2,1)}, u32[]{:S(2)}) copy-start(bf16[128,4,2048]{2,0,1:T(8,128)(2,1)} %all-gather.10.cloned.1.call-done) | copy-start | bytes 6291460
  916.2 144.9 %all-gather.24.cloned.1.call-start = ((), (), s32[]{:S(2)}) async-start(), calls=%async_computation.10 | async-start | bytes 1310720 | tf_op jit(solution)/shard_map/all_gather | solution.py:13
  1046.1 79.0 %all-gather.26.cloned.1.call-start = ((), (), s32[]{:S(2)}) async-start(), calls=%async_computation.11 | async-start | bytes 2359296 | tf_op jit(solution)/shard_map/all_gather | solution.py:104
  1061.1 40.1 %all-to-all-start = ((bf16[128,8,512]{0,2,1:T(8,128)(2,1)}), bf16[128,8,512]{0,2,1:T(8,128)(2,1)S(1)}, u32[]{:S(2)}, u32[]{:S(2)}) async-start(bf16[128,8,512]{0,2,1:T(8,128)(2,1)} %bitcast.57), calls=%async_computation.1 | async-start | bytes 2097152 | tf_op jit(solution)/shard_map/all_to_all | solution.py:100
Sparse Core Ops, SparseCore 0:
  10.1 25.2 all-gather.9
  45.5 280.1 reduce-scatter.1
  453.7 34.2 all-gather.15
  490.5 124.9 all-gather.13
  617.4 123.1 all-gather.11
  742.5 32.6 all-gather.17
  783.2 124.9 all-gather.19
  916.3 123.1 all-gather.21
  1046.2 14.8 all-gather.23
  1063.5 61.5 all-gather.25
where the time goes:
time: 1140 us
  waiting for transfers between devices  932 us (82%)
  blocking collectives  120 us (11%)
  matrix products  54.2 us (5%)
  between operations  14.3 us (1%)
    all_gather x4, waiting for transfers between devices, shared_rows(): return lax.all_gather(piece, ('tok', 'grp'), axis=0, tiled=True)  493 us
    reduce_scatter x1, waiting for transfers between devices, token_sums(): lax.psum_scatter(maker(jnp.int32(0), rows * lax.axis_size(('tok', 'grp'))...  280 us
    psum x3, blocking collectives, shared_total(): return lax.psum(vector, ('tok', 'out', 'grp'))  120 us
    all_gather x4, waiting for transfers between devices, spread(): return lax.all_gather(piece, 'out', axis=2, tiled=True)  108 us
    all_to_all x1, waiting for transfers between devices, local(): lax.all_to_all(acts_whole, ('tok', 'grp'), split_axis=1, concat_axis=0, t...  27.3 us
    dot_general x3, matrix products, multiply(): jnp.einsum('rkj,jkc->rkc', row_band, column_band, preferred_element_type=...  23.8 us
  transfers between devices with their start and end apart: 11, of which 11 were waited for; matrix products, arithmetic and copies ran while one was open for 1% of the time, Pallas kernels for 0%

commit v1 on v0

--- a/solution.py
+++ b/solution.py
@@ -7,6 +7,17 @@
 POWER = 3
 DAMPING = 0.1
 HIGH = lax.Precision.HIGHEST
+
+
+def gather_around(x, axis, dim):
+    ways = lax.axis_size(axis)
+    pieces = [x]
+    for far in range(1, ways):
+        pieces.append(
+            lax.ppermute(pieces[far - 1], axis, [(d, (d - 1) % ways) for d in range(ways)])
+        )
+    line = jnp.concatenate(pieces, axis=dim)
+    return jnp.roll(line, lax.axis_index(axis) * x.shape[dim], axis=dim)
 
 
 def spread(piece):
@@ -23,7 +34,7 @@
 
 
 def shared_rows(piece):
-    return lax.all_gather(piece, ("tok", "grp"), axis=0, tiled=True)
+    return gather_around(piece, ("tok", "grp"), 0)
 
 
 def shared_total(vector):

time: 1140 us -> 1250 us (1.096)
  starting transfers between devices: 6.1 us -> 144 us
  waiting for transfers between devices: 932 us -> 860 us
  local copies, waits for them, and re-layouts: 7.86 us -> 45.8 us
    all_gather x4 -> x0, waiting for transfers between devices: 493 us -> none  [shared_rows(): return lax.all_gather(piece, ('tok', 'grp'), axis=0, tiled=True)]
    ppermute x0 -> x28, waiting for transfers between devices: none -> 482 us  [gather_around(): lax.ppermute(pieces[far - 1], axis, [(d, (d - 1) % ways) for d in range(w...]
    ppermute x0 -> x28, starting transfers between devices: none -> 139 us  [gather_around(): lax.ppermute(pieces[far - 1], axis, [(d, (d - 1) % ways) for d in range(w...]
    all_gather x4, waiting for transfers between devices: 108 us -> 46.9 us  [spread(): return lax.all_gather(piece, 'out', axis=2, tiled=True)]
    unnamed x9 -> x45, local copies, waits for them, and re-layouts: 4.8 us -> 37.2 us
  transfers between devices with their start and end apart: 11 -> 35, of which waited for: 11 -> 33; matrix products, arithmetic and copies ran while one was open for 1% -> 4% of each run, Pallas kernels for 0% -> 0%
where the time goes in v1:
time: 1250 us
  waiting for transfers between devices  860 us (69%)
  starting transfers between devices  144 us (12%)
  blocking collectives  120 us (10%)
  matrix products  60.5 us (5%)
  local copies, waits for them, and re-layouts  45.8 us (4%)
  between operations  14.3 us (1%)
    ppermute x28, waiting for transfers between devices, gather_around(): lax.ppermute(pieces[far - 1], axis, [(d, (d - 1) % ways) for d in range(w...  482 us
    reduce_scatter x1, waiting for transfers between devices, token_sums(): lax.psum_scatter(maker(jnp.int32(0), rows * lax.axis_size(('tok', 'grp'))...  280 us
    ppermute x28, starting transfers between devices, gather_around(): lax.ppermute(pieces[far - 1], axis, [(d, (d - 1) % ways) for d in range(w...  139 us
    psum x3, blocking collectives, shared_total(): return lax.psum(vector, ('tok', 'out', 'grp'))  120 us
    all_gather x4, waiting for transfers between devices, spread(): return lax.all_gather(piece, 'out', axis=2, tiled=True)  46.9 us
    unnamed x45, local copies, waits for them, and re-layouts  37.2 us
    all_to_all x1, waiting for transfers between devices, local(): lax.all_to_all(acts_whole, ('tok', 'grp'), split_axis=1, concat_axis=0, t...  27.3 us
    dot_general x3, matrix products, multiply(): jnp.einsum('rkj,jkc->rkc', row_band, column_band, preferred_element_type=...  25.3 us
  transfers between devices with their start and end apart: 35, of which 33 were waited for; matrix products, arithmetic and copies ran while one was open for 4% of the time, Pallas kernels for 0%

profile of v1, /device:TPU:0, one launch (start us, length us, event | category | flops | bytes accessed | tf_op | source)
XLA Modules:
  0.0 1247.7 jit_solution(4963366044266130684)
XLA Ops:
  10.0 25.4 %all-gather.6.cloned.1.call-done = bf16[128,4,2048]{2,0,1:T(8,128)(2,1)} async-done(((bf16[128,4,512]{2,0,1:T(8,128)(2,1)}), bf16[128,4,2048]{2,0,1:T(8,128)(2,1)}) %all-gather.6.cloned.1.call-update) | async-done | bytes 2097168 | tf_op jit(solution)/shard_map/all_gather | solution.py:24
  35.4 9.9 convolution_bitcast_fusion
  45.6 280.1 %reduce-scatter.2.cloned.1.call-done = f32[256,4,512]{0,2,1:T(8,128)} async-done(((f32[2048,4,512]{0,2,1:T(8,128)}), f32[256,4,512]{0,2,1:T(8,128)}) %reduce-scatter.2.cloned.1.call-update) | async-done | bytes 2097168 | tf_op jit(solution)/shard_map/reduce_scatter | solution.py:28
  328.8 39.4 %psum.21 = f32[4,2048]{1,0:T(4,128)S(1)} all-reduce(f32[4,2048]{1,0:T(4,128)S(1)} %bitcast_dynamic-update-slice_fusion.2), channel_id=1, replica_groups=mesh['tok'=4,'out'=4,'grp'=2] {'tok','out','grp'}, use_global_device_ids=true, to_apply=%region_1.2 | all-reduce | flops 8192 | bytes 65536 | tf_op jit(solution)/shard_map/psum | solution.py:41
  371.4 39.9 %psum.22 = f32[4,2048]{1,0:T(4,128)S(1)} all-reduce(f32[4,2048]{1,0:T(4,128)S(1)} %bitcast_dynamic-update-slice_fusion.1), channel_id=1, replica_groups=mesh['tok'=4,'out'=4,'grp'=2] {'tok','out','grp'}, use_global_device_ids=true, to_apply=%region_3.4 | all-reduce | flops 8192 | bytes 65536 | tf_op jit(solution)/shard_map/psum | solution.py:41
  414.5 40.3 %psum.23 = f32[4,2048]{1,0:T(4,128)S(1)} all-reduce(f32[4,2048]{1,0:T(4,128)S(1)} %bitcast_dynamic-update-slice_fusion), channel_id=1, replica_groups=mesh['tok'=4,'out'=4,'grp'=2] {'tok','out','grp'}, use_global_device_ids=true, to_apply=%region_5.6 | all-reduce | flops 8192 | bytes 65536 | tf_op jit(solution)/shard_map/psum | solution.py:41
  461.5 21.0 %collective-permute-done.7 = bf16[256,4,512]{0,2,1:T(8,128)(2,1)S(1)} collective-permute-done((bf16[256,4,512]{0,2,1:T(8,128)(2,1)}, bf16[256,4,512]{0,2,1:T(8,128)(2,1)S(1)}, u32[]{:S(2)}, u32[]{:S(2)}) %collective-permute-start.7) | collective-permute-done | bytes 1048608 | tf_op jit(solution)/shard_map/ppermute | solution.py:17
  487.7 19.8 %collective-permute-done.8 = bf16[256,4,512]{0,2,1:T(8,128)(2,1)S(1)} collective-permute-done((bf16[256,4,512]{0,2,1:T(8,128)(2,1)S(1)}, bf16[256,4,512]{0,2,1:T(8,128)(2,1)S(1)}, u32[]{:S(2)}, u32[]{:S(2)}) %collective-permute-start.8) | collective-permute-done | bytes 1048608 | tf_op jit(solution)/shard_map/ppermute | solution.py:17
  507.5 5.2 collective-permute-start.9
  512.7 19.0 %collective-permute-done.9 = bf16[256,4,512]{0,2,1:T(8,128)(2,1)S(1)} collective-permute-done((bf16[256,4,512]{0,2,1:T(8,128)(2,1)S(1)}, bf16[256,4,512]{0,2,1:T(8,128)(2,1)S(1)}, u32[]{:S(2)}, u32[]{:S(2)}) %collective-permute-start.9) | collective-permute-done | bytes 1048608 | tf_op jit(solution)/shard_map/ppermute | solution.py:17
  531.7 5.2 collective-permute-start.10
  536.8 18.1 %collective-permute-done.10 = bf16[256,4,512]{0,2,1:T(8,128)(2,1)S(1)} collective-permute-done((bf16[256,4,512]{0,2,1:T(8,128)(2,1)S(1)}, bf16[256,4,512]{0,2,1:T(8,128)(2,1)S(1)}, u32[]{:S(2)}, u32[]{:S(2)}) %collective-permute-start.10) | collective-permute-done | bytes 1048608 | tf_op jit(solution)/shard_map/ppermute | solution.py:17
  555.0 5.2 collective-permute-start.11
  560.2 18.1 %collective-permute-done.11 = bf16[256,4,512]{0,2,1:T(8,128)(2,1)S(1)} collective-permute-done((bf16[256,4,512]{0,2,1:T(8,128)(2,1)S(1)}, bf16[256,4,512]{0,2,1:T(8,128)(2,1)S(1)}, u32[]{:S(2)}, u32[]{:S(2)}) %collective-permute-start.11) | collective-permute-done | bytes 1048608 | tf_op jit(solution)/shard_map/ppermute | solution.py:17
  578.3 5.2 collective-permute-start.12
  583.6 23.5 %collective-permute-done.12 = bf16[256,4,512]{0,2,1:T(8,128)(2,1)} collective-permute-done((bf16[256,4,512]{0,2,1:T(8,128)(2,1)S(1)}, bf16[256,4,512]{0,2,1:T(8,128)(2,1)}, u32[]{:S(2)}, u32[]{:S(2)}) %collective-permute-start.12) | collective-permute-done | bytes 1048608 | tf_op jit(solution)/shard_map/ppermute | solution.py:17
  607.0 5.3 collective-permute-start.13
  612.3 17.3 %collective-permute-done = bf16[256,4,512]{0,2,1:T(8,128)(2,1)S(1)} collective-permute-done((bf16[256,4,512]{0,2,1:T(8,128)(2,1)}, bf16[256,4,512]{0,2,1:T(8,128)(2,1)S(1)}, u32[]{:S(2)}, u32[]{:S(2)}) %collective-permute-start) | collective-permute-done | bytes 1048608 | tf_op jit(solution)/shard_map/ppermute | solution.py:17
  646.2 5.9 collective-permute-done.13
  654.4 9.1 fusion.24
  668.7 5.3 collective-permute-start.2
  674.0 18.5 %collective-permute-done.2 = bf16[256,4,512]{0,2,1:T(8,128)(2,1)S(1)} collective-permute-done((bf16[256,4,512]{0,2,1:T(8,128)(2,1)}, bf16[256,4,512]{0,2,1:T(8,128)(2,1)S(1)}, u32[]{:S(2)}, u32[]{:S(2)}) %collective-permute-start.2) | collective-permute-done | bytes 1048608 | tf_op jit(solution)/shard_map/ppermute | solution.py:17
  697.5 18.1 %collective-permute-done.3 = bf16[256,4,512]{0,2,1:T(8,128)(2,1)S(1)} collective-permute-done((bf16[256,4,512]{0,2,1:T(8,128)(2,1)S(1)}, bf16[256,4,512]{0,2,1:T(8,128)(2,1)S(1)}, u32[]{:S(2)}, u32[]{:S(2)}) %collective-permute-start.3) | collective-permute-done | bytes 1048608 | tf_op jit(solution)/shard_map/ppermute | solution.py:17
  715.7 5.2 collective-permute-start.4
  720.9 18.1 %collective-permute-done.4 = bf16[256,4,512]{0,2,1:T(8,128)(2,1)S(1)} collective-permute-done((bf16[256,4,512]{0,2,1:T(8,128)(2,1)S(1)}, bf16[256,4,512]{0,2,1:T(8,128)(2,1)S(1)}, u32[]{:S(2)}, u32[]{:S(2)}) %collective-permute-start.4) | collective-permute-done | bytes 1048608 | tf_op jit(solution)/shard_map/ppermute | solution.py:17
  739.0 5.2 collective-permute-start.5
  744.2 18.1 %collective-permute-done.5 = bf16[256,4,512]{0,2,1:T(8,128)(2,1)S(1)} collective-permute-done((bf16[256,4,512]{0,2,1:T(8,128)(2,1)S(1)}, bf16[256,4,512]{0,2,1:T(8,128)(2,1)S(1)}, u32[]{:S(2)}, u32[]{:S(2)}) %collective-permute-start.5) | collective-permute-done | bytes 1048608 | tf_op jit(solution)/shard_map/ppermute | solution.py:17
  762.3 5.2 collective-permute-start.6
  781.0 9.0 constant_dynamic-update-slice_fusion.23
  790.0 5.2 collective-permute-start.14
  795.2 19.7 %collective-permute-done.14 = bf16[256,4,512]{0,2,1:T(8,128)(2,1)S(1)} collective-permute-done((bf16[256,4,512]{0,2,1:T(8,128)(2,1)S(1)}, bf16[256,4,512]{0,2,1:T(8,128)(2,1)S(1)}, u32[]{:S(2)}, u32[]{:S(2)}) %collective-permute-start.14) | collective-permute-done | bytes 1048608 | tf_op jit(solution)/shard_map/ppermute | solution.py:17
  815.0 5.2 collective-permute-start.15
  820.1 20.9 %collective-permute-done.15 = bf16[256,4,512]{0,2,1:T(8,128)(2,1)S(1)} collective-permute-done((bf16[256,4,512]{0,2,1:T(8,128)(2,1)S(1)}, bf16[256,4,512]{0,2,1:T(8,128)(2,1)S(1)}, u32[]{:S(2)}, u32[]{:S(2)}) %collective-permute-start.15) | collective-permute-done | bytes 1048608 | tf_op jit(solution)/shard_map/ppermute | solution.py:17
  841.0 5.2 collective-permute-start.16
  846.2 22.0 %collective-permute-done.16 = bf16[256,4,512]{0,2,1:T(8,128)(2,1)S(1)} collective-permute-done((bf16[256,4,512]{0,2,1:T(8,128)(2,1)S(1)}, bf16[256,4,512]{0,2,1:T(8,128)(2,1)S(1)}, u32[]{:S(2)}, u32[]{:S(2)}) %collective-permute-start.16) | collective-permute-done | bytes 1048608 | tf_op jit(solution)/shard_map/ppermute | solution.py:17
  868.2 5.2 collective-permute-start.17
  873.4 23.2 %collective-permute-done.17 = bf16[256,4,512]{0,2,1:T(8,128)(2,1)S(1)} collective-permute-done((bf16[256,4,512]{0,2,1:T(8,128)(2,1)S(1)}, bf16[256,4,512]{0,2,1:T(8,128)(2,1)S(1)}, u32[]{:S(2)}, u32[]{:S(2)}) %collective-permute-start.17) | collective-permute-done | bytes 1048608 | tf_op jit(solution)/shard_map/ppermute | solution.py:17
  896.6 5.2 collective-permute-start.18
  901.8 22.8 %collective-permute-done.18 = bf16[256,4,512]{0,2,1:T(8,128)(2,1)S(1)} collective-permute-done((bf16[256,4,512]{0,2,1:T(8,128)(2,1)S(1)}, bf16[256,4,512]{0,2,1:T(8,128)(2,1)S(1)}, u32[]{:S(2)}, u32[]{:S(2)}) %collective-permute-start.18) | collective-permute-done | bytes 1048608 | tf_op jit(solution)/shard_map/ppermute | solution.py:17
  924.6 5.2 collective-permute-start.19
  929.7 21.9 %collective-permute-done.19 = bf16[256,4,512]{0,2,1:T(8,128)(2,1)S(1)} collective-permute-done((bf16[256,4,512]{0,2,1:T(8,128)(2,1)S(1)}, bf16[256,4,512]{0,2,1:T(8,128)(2,1)S(1)}, u32[]{:S(2)}, u32[]{:S(2)}) %collective-permute-start.19) | collective-permute-done | bytes 1048608 | tf_op jit(solution)/shard_map/ppermute | solution.py:17
  951.7 5.2 collective-permute-start.20
  963.4 11.2 collective-permute-done.20
  975.8 7.2 constant_dynamic-update-slice_fusion.31
  982.9 5.1 collective-permute-start.21
  988.1 19.9 %collective-permute-done.21 = bf16[256,4,512]{2,0,1:T(8,128)(2,1)S(1)} collective-permute-done((bf16[256,4,512]{2,0,1:T(8,128)(2,1)S(1)}, bf16[256,4,512]{2,0,1:T(8,128)(2,1)S(1)}, u32[]{:S(2)}, u32[]{:S(2)}) %collective-permute-start.21) | collective-permute-done | bytes 1048608 | tf_op jit(solution)/shard_map/ppermute | solution.py:17
  1008.0 5.2 collective-permute-start.22
  1013.1 19.1 %collective-permute-done.22 = bf16[256,4,512]{2,0,1:T(8,128)(2,1)S(1)} collective-permute-done((bf16[256,4,512]{2,0,1:T(8,128)(2,1)S(1)}, bf16[256,4,512]{2,0,1:T(8,128)(2,1)S(1)}, u32[]{:S(2)}, u32[]{:S(2)}) %collective-permute-start.22) | collective-permute-done | bytes 1048608 | tf_op jit(solution)/shard_map/ppermute | solution.py:17
  1032.2 5.2 collective-permute-start.23
  1037.4 18.2 %collective-permute-done.23 = bf16[256,4,512]{2,0,1:T(8,128)(2,1)S(1)} collective-permute-done((bf16[256,4,512]{2,0,1:T(8,128)(2,1)S(1)}, bf16[256,4,512]{2,0,1:T(8,128)(2,1)S(1)}, u32[]{:S(2)}, u32[]{:S(2)}) %collective-permute-start.23) | collective-permute-done | bytes 1048608 | tf_op jit(solution)/shard_map/ppermute | solution.py:17
  1055.6 5.2 collective-permute-start.24
  1060.8 18.1 %collective-permute-done.24 = bf16[256,4,512]{2,0,1:T(8,128)(2,1)S(1)} collective-permute-done((bf16[256,4,512]{2,0,1:T(8,128)(2,1)S(1)}, bf16[256,4,512]{2,0,1:T(8,128)(2,1)S(1)}, u32[]{:S(2)}, u32[]{:S(2)}) %collective-permute-start.24) | collective-permute-done | bytes 1048608 | tf_op jit(solution)/shard_map/ppermute | solution.py:17
  1078.9 5.2 collective-permute-start.25
  1084.1 18.1 %collective-permute-done.25 = bf16[256,4,512]{2,0,1:T(8,128)(2,1)S(1)} collective-permute-done((bf16[256,4,512]{2,0,1:T(8,128)(2,1)S(1)}, bf16[256,4,512]{2,0,1:T(8,128)(2,1)S(1)}, u32[]{:S(2)}, u32[]{:S(2)}) %collective-permute-start.25) | collective-permute-done | bytes 1048608 | tf_op jit(solution)/shard_map/ppermute | solution.py:17
  1102.2 5.2 collective-permute-start.26
  1107.4 15.6 %collective-permute-done.26 = bf16[256,4,512]{2,0,1:T(8,128)(2,1)S(1)} collective-permute-done((bf16[256,4,512]{2,0,1:T(8,128)(2,1)S(1)}, bf16[256,4,512]{2,0,1:T(8,128)(2,1)S(1)}, u32[]{:S(2)}, u32[]{:S(2)}) %collective-permute-start.26) | collective-permute-done | bytes 1048608 | tf_op jit(solution)/shard_map/ppermute | solution.py:17
  1123.0 5.2 collective-permute-start.27
  1134.5 6.0 collective-permute-done.27
  1141.6 7.3 fusion.37
  1150.3 21.5 %all-gather.12.cloned.1.call-done = bf16[128,2,2048]{0,2,1:T(8,128)(2,1)} async-done(((bf16[128,2,512]{0,2,1:T(8,128)(2,1)}), bf16[128,2,2048]{0,2,1:T(8,128)(2,1)}) %all-gather.12.cloned.1.call-update) | async-done | bytes 1048592 | tf_op jit(solution)/shard_map/all_gather | solution.py:24
  1171.9 5.5 all-to-all-start
  1177.4 6.3 fusion.43
  1184.6 27.3 %all-to-all-done = bf16[128,8,512]{0,2,1:T(8,128)(2,1)S(1)} async-done(((bf16[128,8,512]{0,2,1:T(8,128)(2,1)}), bf16[128,8,512]{0,2,1:T(8,128)(2,1)S(1)}, u32[]{:S(2)}, u32[]{:S(2)}) %all-to-all-start) | async-done | bytes 1048608 | tf_op jit(solution)/shard_map/all_to_all | solution.py:111
  1213.1 22.7 %all-gather.14.cloned.1.call-done = bf16[1024,2,512]{0,2,1:T(8,128)(2,1)} async-done(((bf16[128,2,512]{0,2,1:T(8,128)(2,1)}), bf16[1024,2,512]{0,2,1:T(8,128)(2,1)}) %all-gather.14.cloned.1.call-update) | async-done | bytes 2097168 | tf_op jit(solution)/shard_map/all_gather | solution.py:115
  (97 shorter events, 90.4 us)
Async XLA Ops:
  7.2 28.3 %all-gather.6.cloned.1.call-start = ((), (), s32[]{:S(2)}) async-start(), calls=%async_computation.2 | async-start | bytes 2621440 | tf_op jit(solution)/shard_map/all_gather | solution.py:24
  9.2 0.8 copy-start.1
  10.0 315.7 %reduce-scatter.2.cloned.1.call-start = ((), (), s32[]{:S(2)}) async-start(), calls=%async_computation.3 | async-start | bytes 18874368 | tf_op jit(solution)/shard_map/reduce_scatter | solution.py:28
  45.4 609.0 %all-gather.8.cloned.1.call-start = ((), (), s32[]{:S(2)}) async-start(), calls=%async_computation.4 | async-start | bytes 5242880 | tf_op jit(solution)/shard_map/all_gather | solution.py:24
  325.7 129.3 %copy-start = (f32[256,4,512]{0,2,1:T(8,128)S(1)}, f32[256,4,512]{0,2,1:T(8,128)}, u32[]{:S(2)}) copy-start(f32[256,4,512]{0,2,1:T(8,128)} %reduce-scatter.2.cloned.1.call-done) | copy-start | bytes 6291460
  457.5 25.1 %collective-permute-start.7 = (bf16[256,4,512]{0,2,1:T(8,128)(2,1)}, bf16[256,4,512]{0,2,1:T(8,128)(2,1)S(1)}, u32[]{:S(2)}, u32[]{:S(2)}) collective-permute-start(bf16[256,4,512]{0,2,1:T(8,128)(2,1)} %get-tuple-element.16), channel_id=1, source_target_pairs={{0,25},{1,0},{8,1},{9,8},{16,9},{17,16},{24,17},{25,24},{2,27},{3,... | collective-permute-start | bytes 3145736 | tf_op jit(solution)/shard_map/ppermute | solution.py:17
  482.6 24.9 %collective-permute-start.8 = (bf16[256,4,512]{0,2,1:T(8,128)(2,1)S(1)}, bf16[256,4,512]{0,2,1:T(8,128)(2,1)S(1)}, u32[]{:S(2)}, u32[]{:S(2)}) collective-permute-start(bf16[256,4,512]{0,2,1:T(8,128)(2,1)S(1)} %collective-permute-done.7), channel_id=1, source_target_pairs={{0,25},{1,0},{8,1},{9,8},{16,9},{17,16},{24,17},{25,24},{2,27},{3,... | collective-permute-start | bytes 3145736 | tf_op jit(solution)/shard_map/ppermute | solution.py:17
  487.7 293.3 %all-gather.10.cloned.1.call-start = ((), (), s32[]{:S(2)}) async-start(), calls=%async_computation.5 | async-start | bytes 5242880 | tf_op jit(solution)/shard_map/all_gather | solution.py:24
  507.5 76.0 %copy-start.3 = (bf16[256,4,512]{0,2,1:T(8,128)(2,1)}, bf16[256,4,512]{0,2,1:T(8,128)(2,1)S(1)}, u32[]{:S(2)}) copy-start(bf16[256,4,512]{0,2,1:T(8,128)(2,1)S(1)} %collective-permute-done.8) | copy-start | bytes 3145732
  507.5 24.2 %collective-permute-start.9 = (bf16[256,4,512]{0,2,1:T(8,128)(2,1)S(1)}, bf16[256,4,512]{0,2,1:T(8,128)(2,1)S(1)}, u32[]{:S(2)}, u32[]{:S(2)}) collective-permute-start(bf16[256,4,512]{0,2,1:T(8,128)(2,1)S(1)} %collective-permute-done.8), channel_id=1, source_target_pairs={{0,25},{1,0},{8,1},{9,8},{16,9},{17,16},{24,17},{25,24},{2,27},{3,... | collective-permute-start | bytes 3145736 | tf_op jit(solution)/shard_map/ppermute | solution.py:17
  531.6 51.8 %copy-start.4 = (bf16[256,4,512]{0,2,1:T(8,128)(2,1)}, bf16[256,4,512]{0,2,1:T(8,128)(2,1)S(1)}, u32[]{:S(2)}) copy-start(bf16[256,4,512]{0,2,1:T(8,128)(2,1)S(1)} %collective-permute-done.9) | copy-start | bytes 3145732
  531.7 23.3 %collective-permute-start.10 = (bf16[256,4,512]{0,2,1:T(8,128)(2,1)S(1)}, bf16[256,4,512]{0,2,1:T(8,128)(2,1)S(1)}, u32[]{:S(2)}, u32[]{:S(2)}) collective-permute-start(bf16[256,4,512]{0,2,1:T(8,128)(2,1)S(1)} %collective-permute-done.9), channel_id=1, source_target_pairs={{0,25},{1,0},{8,1},{9,8},{16,9},{17,16},{24,17},{25,24},{2,27},{3,... | collective-permute-start | bytes 3145736 | tf_op jit(solution)/shard_map/ppermute | solution.py:17
  555.0 28.6 %copy-start.5 = (bf16[256,4,512]{0,2,1:T(8,128)(2,1)}, bf16[256,4,512]{0,2,1:T(8,128)(2,1)S(1)}, u32[]{:S(2)}) copy-start(bf16[256,4,512]{0,2,1:T(8,128)(2,1)S(1)} %collective-permute-done.10) | copy-start | bytes 3145732
  555.0 23.3 %collective-permute-start.11 = (bf16[256,4,512]{0,2,1:T(8,128)(2,1)S(1)}, bf16[256,4,512]{0,2,1:T(8,128)(2,1)S(1)}, u32[]{:S(2)}, u32[]{:S(2)}) collective-permute-start(bf16[256,4,512]{0,2,1:T(8,128)(2,1)S(1)} %collective-permute-done.10), channel_id=1, source_target_pairs={{0,25},{1,0},{8,1},{9,8},{16,9},{17,16},{24,17},{25,24},{2,27},{3,... | collective-permute-start | bytes 3145736 | tf_op jit(solution)/shard_map/ppermute | solution.py:17
  578.3 28.7 %copy-start.6 = (bf16[256,4,512]{0,2,1:T(8,128)(2,1)}, bf16[256,4,512]{0,2,1:T(8,128)(2,1)S(1)}, u32[]{:S(2)}) copy-start(bf16[256,4,512]{0,2,1:T(8,128)(2,1)S(1)} %collective-permute-done.11) | copy-start | bytes 3145732
  578.3 28.7 %collective-permute-start.12 = (bf16[256,4,512]{0,2,1:T(8,128)(2,1)S(1)}, bf16[256,4,512]{0,2,1:T(8,128)(2,1)}, u32[]{:S(2)}, u32[]{:S(2)}) collective-permute-start(bf16[256,4,512]{0,2,1:T(8,128)(2,1)S(1)} %collective-permute-done.11), channel_id=1, source_target_pairs={{0,25},{1,0},{8,1},{9,8},{16,9},{17,16},{24,17},{25,24},{2,27},{3,... | collective-permute-start | bytes 3145736 | tf_op jit(solution)/shard_map/ppermute | solution.py:17
  583.5 46.1 %collective-permute-start = (bf16[256,4,512]{0,2,1:T(8,128)(2,1)}, bf16[256,4,512]{0,2,1:T(8,128)(2,1)S(1)}, u32[]{:S(2)}, u32[]{:S(2)}) collective-permute-start(bf16[256,4,512]{0,2,1:T(8,128)(2,1)} %get-tuple-element.12), channel_id=1, source_target_pairs={{0,25},{1,0},{8,1},{9,8},{16,9},{17,16},{24,17},{25,24},{2,27},{3,... | collective-permute-start | bytes 3145736 | tf_op jit(solution)/shard_map/ppermute | solution.py:17
  607.0 45.0 %collective-permute-start.13 = (bf16[256,4,512]{0,2,1:T(8,128)(2,1)}, bf16[256,4,512]{0,2,1:T(8,128)(2,1)}, u32[]{:S(2)}, u32[]{:S(2)}) collective-permute-start(bf16[256,4,512]{0,2,1:T(8,128)(2,1)} %collective-permute-done.12), channel_id=1, source_target_pairs={{0,25},{1,0},{8,1},{9,8},{16,9},{17,16},{24,17},{25,24},{2,27},{3,... | collective-permute-start | bytes 3145736 | tf_op jit(solution)/shard_map/ppermute | solution.py:17
  612.3 30.4 %copy-start.7 = (bf16[256,4,512]{0,2,1:T(8,128)(2,1)S(1)}, bf16[256,4,512]{0,2,1:T(8,128)(2,1)}, u32[]{:S(2)}) copy-start(bf16[256,4,512]{0,2,1:T(8,128)(2,1)} %copy-done.6) | copy-start | bytes 3145732
  629.6 39.1 %collective-permute-start.1 = (bf16[256,4,512]{0,2,1:T(8,128)(2,1)S(1)}, bf16[256,4,512]{0,2,1:T(8,128)(2,1)}, u32[]{:S(2)}, u32[]{:S(2)}) collective-permute-start(bf16[256,4,512]{0,2,1:T(8,128)(2,1)S(1)} %collective-permute-done), channel_id=1, source_target_pairs={{0,25},{1,0},{8,1},{9,8},{16,9},{17,16},{24,17},{25,24},{2,27},{3,... | collective-permute-start | bytes 3145736 | tf_op jit(solution)/shard_map/ppermute | solution.py:17
  663.6 508.3 %all-gather.12.cloned.1.call-start = ((), (), s32[]{:S(2)}) async-start(), calls=%async_computation.6 | async-start | bytes 1310720 | tf_op jit(solution)/shard_map/all_gather | solution.py:24
  668.7 23.7 %collective-permute-start.2 = (bf16[256,4,512]{0,2,1:T(8,128)(2,1)}, bf16[256,4,512]{0,2,1:T(8,128)(2,1)S(1)}, u32[]{:S(2)}, u32[]{:S(2)}) collective-permute-start(bf16[256,4,512]{0,2,1:T(8,128)(2,1)} %collective-permute-done.1), channel_id=1, source_target_pairs={{0,25},{1,0},{8,1},{9,8},{16,9},{17,16},{24,17},{25,24},{2,27},{3,... | collective-permute-start | bytes 3145736 | tf_op jit(solution)/shard_map/ppermute | solution.py:17
  692.5 23.2 %collective-permute-start.3 = (bf16[256,4,512]{0,2,1:T(8,128)(2,1)S(1)}, bf16[256,4,512]{0,2,1:T(8,128)(2,1)S(1)}, u32[]{:S(2)}, u32[]{:S(2)}) collective-permute-start(bf16[256,4,512]{0,2,1:T(8,128)(2,1)S(1)} %collective-permute-done.2), channel_id=1, source_target_pairs={{0,25},{1,0},{8,1},{9,8},{16,9},{17,16},{24,17},{25,24},{2,27},{3,... | collective-permute-start | bytes 3145736 | tf_op jit(solution)/shard_map/ppermute | solution.py:17
  715.7 23.3 %collective-permute-start.4 = (bf16[256,4,512]{0,2,1:T(8,128)(2,1)S(1)}, bf16[256,4,512]{0,2,1:T(8,128)(2,1)S(1)}, u32[]{:S(2)}, u32[]{:S(2)}) collective-permute-start(bf16[256,4,512]{0,2,1:T(8,128)(2,1)S(1)} %collective-permute-done.3), channel_id=1, source_target_pairs={{0,25},{1,0},{8,1},{9,8},{16,9},{17,16},{24,17},{25,24},{2,27},{3,... | collective-permute-start | bytes 3145736 | tf_op jit(solution)/shard_map/ppermute | solution.py:17
  739.0 23.3 %collective-permute-start.5 = (bf16[256,4,512]{0,2,1:T(8,128)(2,1)S(1)}, bf16[256,4,512]{0,2,1:T(8,128)(2,1)S(1)}, u32[]{:S(2)}, u32[]{:S(2)}) collective-permute-start(bf16[256,4,512]{0,2,1:T(8,128)(2,1)S(1)} %collective-permute-done.4), channel_id=1, source_target_pairs={{0,25},{1,0},{8,1},{9,8},{16,9},{17,16},{24,17},{25,24},{2,27},{3,... | collective-permute-start | bytes 3145736 | tf_op jit(solution)/shard_map/ppermute | solution.py:17
  762.3 17.5 %collective-permute-start.6 = (bf16[256,4,512]{0,2,1:T(8,128)(2,1)S(1)}, bf16[256,4,512]{0,2,1:T(8,128)(2,1)S(1)}, u32[]{:S(2)}, u32[]{:S(2)}) collective-permute-start(bf16[256,4,512]{0,2,1:T(8,128)(2,1)S(1)} %collective-permute-done.5), channel_id=1, source_target_pairs={{0,25},{1,0},{8,1},{9,8},{16,9},{17,16},{24,17},{25,24},{2,27},{3,... | collective-permute-start | bytes 3145736 | tf_op jit(solution)/shard_map/ppermute | solution.py:17
  790.0 185.7 %copy-start.8 = (bf16[256,4,2048]{0,2,1:T(8,128)(2,1)S(1)}, bf16[256,4,2048]{0,2,1:T(8,128)(2,1)}, u32[]{:S(2)}) copy-start(bf16[256,4,2048]{0,2,1:T(8,128)(2,1)} %all-gather.8.cloned.1.call-done) | copy-start | bytes 12582916
  790.0 24.9 %collective-permute-start.14 = (bf16[256,4,512]{0,2,1:T(8,128)(2,1)S(1)}, bf16[256,4,512]{0,2,1:T(8,128)(2,1)S(1)}, u32[]{:S(2)}, u32[]{:S(2)}) collective-permute-start(bf16[256,4,512]{0,2,1:T(8,128)(2,1)S(1)} %get-tuple-element.22), channel_id=1, source_target_pairs={{0,25},{1,0},{8,1},{9,8},{16,9},{17,16},{24,17},{25,24},{2,27},{3,... | collective-permute-start | bytes 3145736 | tf_op jit(solution)/shard_map/ppermute | solution.py:17
  815.0 26.1 %collective-permute-start.15 = (bf16[256,4,512]{0,2,1:T(8,128)(2,1)S(1)}, bf16[256,4,512]{0,2,1:T(8,128)(2,1)S(1)}, u32[]{:S(2)}, u32[]{:S(2)}) collective-permute-start(bf16[256,4,512]{0,2,1:T(8,128)(2,1)S(1)} %collective-permute-done.14), channel_id=1, source_target_pairs={{0,25},{1,0},{8,1},{9,8},{16,9},{17,16},{24,17},{25,24},{2,27},{3,... | collective-permute-start | bytes 3145736 | tf_op jit(solution)/shard_map/ppermute | solution.py:17
  841.0 27.2 %collective-permute-start.16 = (bf16[256,4,512]{0,2,1:T(8,128)(2,1)S(1)}, bf16[256,4,512]{0,2,1:T(8,128)(2,1)S(1)}, u32[]{:S(2)}, u32[]{:S(2)}) collective-permute-start(bf16[256,4,512]{0,2,1:T(8,128)(2,1)S(1)} %collective-permute-done.15), channel_id=1, source_target_pairs={{0,25},{1,0},{8,1},{9,8},{16,9},{17,16},{24,17},{25,24},{2,27},{3,... | collective-permute-start | bytes 3145736 | tf_op jit(solution)/shard_map/ppermute | solution.py:17
  868.2 28.4 %collective-permute-start.17 = (bf16[256,4,512]{0,2,1:T(8,128)(2,1)S(1)}, bf16[256,4,512]{0,2,1:T(8,128)(2,1)S(1)}, u32[]{:S(2)}, u32[]{:S(2)}) collective-permute-start(bf16[256,4,512]{0,2,1:T(8,128)(2,1)S(1)} %collective-permute-done.16), channel_id=1, source_target_pairs={{0,25},{1,0},{8,1},{9,8},{16,9},{17,16},{24,17},{25,24},{2,27},{3,... | collective-permute-start | bytes 3145736 | tf_op jit(solution)/shard_map/ppermute | solution.py:17
  896.6 27.9 %collective-permute-start.18 = (bf16[256,4,512]{0,2,1:T(8,128)(2,1)S(1)}, bf16[256,4,512]{0,2,1:T(8,128)(2,1)S(1)}, u32[]{:S(2)}, u32[]{:S(2)}) collective-permute-start(bf16[256,4,512]{0,2,1:T(8,128)(2,1)S(1)} %collective-permute-done.17), channel_id=1, source_target_pairs={{0,25},{1,0},{8,1},{9,8},{16,9},{17,16},{24,17},{25,24},{2,27},{3,... | collective-permute-start | bytes 3145736 | tf_op jit(solution)/shard_map/ppermute | solution.py:17
  924.6 27.1 %collective-permute-start.19 = (bf16[256,4,512]{0,2,1:T(8,128)(2,1)S(1)}, bf16[256,4,512]{0,2,1:T(8,128)(2,1)S(1)}, u32[]{:S(2)}, u32[]{:S(2)}) collective-permute-start(bf16[256,4,512]{0,2,1:T(8,128)(2,1)S(1)} %collective-permute-done.18), channel_id=1, source_target_pairs={{0,25},{1,0},{8,1},{9,8},{16,9},{17,16},{24,17},{25,24},{2,27},{3,... | collective-permute-start | bytes 3145736 | tf_op jit(solution)/shard_map/ppermute | solution.py:17
  951.7 23.0 %collective-permute-start.20 = (bf16[256,4,512]{0,2,1:T(8,128)(2,1)S(1)}, bf16[256,4,512]{0,2,1:T(8,128)(2,1)S(1)}, u32[]{:S(2)}, u32[]{:S(2)}) collective-permute-start(bf16[256,4,512]{0,2,1:T(8,128)(2,1)S(1)} %collective-permute-done.19), channel_id=1, source_target_pairs={{0,25},{1,0},{8,1},{9,8},{16,9},{17,16},{24,17},{25,24},{2,27},{3,... | collective-permute-start | bytes 3145736 | tf_op jit(solution)/shard_map/ppermute | solution.py:17
  982.9 158.7 %copy-start.2 = (bf16[128,4,2048]{2,0,1:T(8,128)(2,1)S(1)}, bf16[128,4,2048]{2,0,1:T(8,128)(2,1)}, u32[]{:S(2)}) copy-start(bf16[128,4,2048]{2,0,1:T(8,128)(2,1)} %all-gather.6.cloned.1.call-done) | copy-start | bytes 6291460
  982.9 25.0 %collective-permute-start.21 = (bf16[256,4,512]{2,0,1:T(8,128)(2,1)S(1)}, bf16[256,4,512]{2,0,1:T(8,128)(2,1)S(1)}, u32[]{:S(2)}, u32[]{:S(2)}) collective-permute-start(bf16[256,4,512]{2,0,1:T(8,128)(2,1)S(1)} %get-tuple-element.24), channel_id=1, source_target_pairs={{0,25},{1,0},{8,1},{9,8},{16,9},{17,16},{24,17},{25,24},{2,27},{3,... | collective-permute-start | bytes 3145736 | tf_op jit(solution)/shard_map/ppermute | solution.py:17
  1008.0 24.2 %collective-permute-start.22 = (bf16[256,4,512]{2,0,1:T(8,128)(2,1)S(1)}, bf16[256,4,512]{2,0,1:T(8,128)(2,1)S(1)}, u32[]{:S(2)}, u32[]{:S(2)}) collective-permute-start(bf16[256,4,512]{2,0,1:T(8,128)(2,1)S(1)} %collective-permute-done.21), channel_id=1, source_target_pairs={{0,25},{1,0},{8,1},{9,8},{16,9},{17,16},{24,17},{25,24},{2,27},{3,... | collective-permute-start | bytes 3145736 | tf_op jit(solution)/shard_map/ppermute | solution.py:17
  1032.2 23.4 %collective-permute-start.23 = (bf16[256,4,512]{2,0,1:T(8,128)(2,1)S(1)}, bf16[256,4,512]{2,0,1:T(8,128)(2,1)S(1)}, u32[]{:S(2)}, u32[]{:S(2)}) collective-permute-start(bf16[256,4,512]{2,0,1:T(8,128)(2,1)S(1)} %collective-permute-done.22), channel_id=1, source_target_pairs={{0,25},{1,0},{8,1},{9,8},{16,9},{17,16},{24,17},{25,24},{2,27},{3,... | collective-permute-start | bytes 3145736 | tf_op jit(solution)/shard_map/ppermute | solution.py:17
  1055.6 23.3 %collective-permute-start.24 = (bf16[256,4,512]{2,0,1:T(8,128)(2,1)S(1)}, bf16[256,4,512]{2,0,1:T(8,128)(2,1)S(1)}, u32[]{:S(2)}, u32[]{:S(2)}) collective-permute-start(bf16[256,4,512]{2,0,1:T(8,128)(2,1)S(1)} %collective-permute-done.23), channel_id=1, source_target_pairs={{0,25},{1,0},{8,1},{9,8},{16,9},{17,16},{24,17},{25,24},{2,27},{3,... | collective-permute-start | bytes 3145736 | tf_op jit(solution)/shard_map/ppermute | solution.py:17
  1078.9 23.3 %collective-permute-start.25 = (bf16[256,4,512]{2,0,1:T(8,128)(2,1)S(1)}, bf16[256,4,512]{2,0,1:T(8,128)(2,1)S(1)}, u32[]{:S(2)}, u32[]{:S(2)}) collective-permute-start(bf16[256,4,512]{2,0,1:T(8,128)(2,1)S(1)} %collective-permute-done.24), channel_id=1, source_target_pairs={{0,25},{1,0},{8,1},{9,8},{16,9},{17,16},{24,17},{25,24},{2,27},{3,... | collective-permute-start | bytes 3145736 | tf_op jit(solution)/shard_map/ppermute | solution.py:17
  1102.2 20.8 %collective-permute-start.26 = (bf16[256,4,512]{2,0,1:T(8,128)(2,1)S(1)}, bf16[256,4,512]{2,0,1:T(8,128)(2,1)S(1)}, u32[]{:S(2)}, u32[]{:S(2)}) collective-permute-start(bf16[256,4,512]{2,0,1:T(8,128)(2,1)S(1)} %collective-permute-done.25), channel_id=1, source_target_pairs={{0,25},{1,0},{8,1},{9,8},{16,9},{17,16},{24,17},{25,24},{2,27},{3,... | collective-permute-start | bytes 3145736 | tf_op jit(solution)/shard_map/ppermute | solution.py:17
  1123.0 17.5 %collective-permute-start.27 = (bf16[256,4,512]{2,0,1:T(8,128)(2,1)S(1)}, bf16[256,4,512]{2,0,1:T(8,128)(2,1)S(1)}, u32[]{:S(2)}, u32[]{:S(2)}) collective-permute-start(bf16[256,4,512]{2,0,1:T(8,128)(2,1)S(1)} %collective-permute-done.26), channel_id=1, source_target_pairs={{0,25},{1,0},{8,1},{9,8},{16,9},{17,16},{24,17},{25,24},{2,27},{3,... | collective-permute-start | bytes 3145736 | tf_op jit(solution)/shard_map/ppermute | solution.py:17
  1149.8 86.1 %all-gather.14.cloned.1.call-start = ((), (), s32[]{:S(2)}) async-start(), calls=%async_computation.7 | async-start | bytes 2359296 | tf_op jit(solution)/shard_map/all_gather | solution.py:115
  1171.9 40.1 %all-to-all-start = ((bf16[128,8,512]{0,2,1:T(8,128)(2,1)}), bf16[128,8,512]{0,2,1:T(8,128)(2,1)S(1)}, u32[]{:S(2)}, u32[]{:S(2)}) async-start(bf16[128,8,512]{0,2,1:T(8,128)(2,1)} %bitcast.53), calls=%async_computation.1 | async-start | bytes 2097152 | tf_op jit(solution)/shard_map/all_to_all | solution.py:111
Sparse Core Ops, SparseCore 0:
  10.1 25.2 all-gather.5
  45.5 280.1 reduce-scatter.1
  487.8 31.7 all-gather.7
  663.7 39.5 all-gather.9
  1149.9 21.9 all-gather.11
  1174.3 61.5 all-gather.13
